TPU v7x, 32 devices: a whole 2x2x4 slice. The times are simulated.
32 devices in a mesh: fsdp: 4 (over y, x), seq: 8 (over z, core).
Axes of the slice: x: 2, y: 2, z: 4, core: 2. Of those that a mesh axis runs over, the one named last changes fastest.
Arguments:
- images: bfloat16 [32, 1024, 1152], P('fsdp', 'seq'), may hold values from -8 to 8
- lengths: int32 [32], P('fsdp'), may hold values from 256 to 1024
- ln1_gain: bfloat16 [1152], P('fsdp'), may hold values from 0.099609375 to 1.8984375
- ln1_bias: bfloat16 [1152], P('fsdp'), may hold values from -3 to 3
- w_qkv: bfloat16 [1152, 3456], P('fsdp'), may hold values from -1 to 1
- qv_bias: bfloat16 [2, 1152], P(None, 'fsdp'), may hold values from -3 to 3
- w_out: bfloat16 [1152, 1152], P('fsdp'), may hold values from -0.75 to 0.75
- out_bias: bfloat16 [1152], P('fsdp'), may hold values from -3 to 3
- ln2_gain: bfloat16 [1152], P('fsdp'), may hold values from 0.099609375 to 1.8984375
- ln2_bias: bfloat16 [1152], P('fsdp'), may hold values from -3 to 3
- w_up: bfloat16 [1152, 4304], P('fsdp'), may hold values from -0.1875 to 0.1875
- up_bias: bfloat16 [4304], P('fsdp'), may hold values from -3 to 3
- w_down: bfloat16 [4304, 1152], P(None, 'fsdp'), may hold values from -0.09375 to 0.09375
- down_bias: bfloat16 [1152], P('fsdp'), may hold values from -3 to 3
- cotangent: bfloat16 [32, 1024, 1152], P('fsdp', 'seq'), may hold values from -6 to 6
Outputs:
- layer_out: bfloat16 [32, 1024, 1152], P('fsdp', 'seq')
- grad_images: bfloat16 [32, 1024, 1152], P('fsdp', 'seq')
- grad_ln1_gain: float32 [1152], P('fsdp')
- grad_ln1_bias: float32 [1152], P('fsdp')
- grad_w_qkv: float32 [1152, 3456], P('fsdp')
- grad_qv_bias: float32 [2, 1152], P(None, 'fsdp')
- grad_w_out: float32 [1152, 1152], P('fsdp')
- grad_out_bias: float32 [1152], P('fsdp')
- grad_ln2_gain: float32 [1152], P('fsdp')
- grad_ln2_bias: float32 [1152], P('fsdp')
- grad_w_up: float32 [1152, 4304], P('fsdp')
- grad_up_bias: float32 [4304], P('fsdp')
- grad_w_down: float32 [4304, 1152], P(None, 'fsdp')
- grad_down_bias: float32 [1152], P('fsdp')
All inputs are finite; a program needn't handle non-finite values.
Results may differ from a plain program's by a relative error of at most 0.017.
Values may be sent and summed in bfloat16 or wider, within the bound.
A program may use at most 256 MiB of HBM per device.

v0:
```python
import jax
import jax.numpy as jnp
from jax import lax
from jax.sharding import PartitionSpec as P

H = 16
HD = 72
epsilon = 1e-06
wide_block = 1024


def for_sending(shard):

    def short(part):
        return part.astype(jnp.bfloat16) if part.dtype == jnp.float32 else part

    return jax.tree.map(short, shard)


def normalize(field, gain_vec, bias_vec):
    center_mean = jnp.mean(field, -1, keepdims=True)
    centered = field - center_mean
    variance = jnp.mean(centered * centered, -1, keepdims=True)
    return centered * lax.rsqrt(variance + epsilon) * gain_vec + bias_vec


def gelu_tanh(field):
    return jax.nn.gelu(field, approximate=True)


def attend_item(queries, keys_all, values, length_one):
    length_all = keys_all.shape[1]
    block_rows = min(wide_block, length_all)
    visible = (jnp.arange(length_all) < length_one)[None, :]
    pieces = []
    log_sums = []
    for offset in range(0, length_all, block_rows):
        scores = jnp.einsum(
            "dq,dk->qk",
            queries[:, offset : offset + block_rows],
            keys_all,
            preferred_element_type=jnp.float32,
        )
        scores = jnp.where(visible, scores, -1e30)
        row_max = jnp.max(scores, -1, keepdims=True)
        exponents = jnp.exp(scores - row_max)
        denominator = jnp.sum(exponents, -1, keepdims=True)
        softmax_low = (exponents / denominator).astype(jnp.bfloat16)
        pieces.append(
            jnp.einsum("qk,dk->dq", softmax_low, values, preferred_element_type=jnp.float32)
        )
        log_sums.append(row_max[:, 0] + jnp.log(denominator[:, 0]))
    return (jnp.concatenate(pieces, 1).astype(jnp.bfloat16), jnp.concatenate(log_sums, 0))


def attend_back(queries, keys_all, values, length_one, log_sum, grad_mixed):
    length_all = keys_all.shape[1]
    block_rows = min(wide_block, length_all)
    visible = (jnp.arange(length_all) < length_one)[None, :]
    grad_keys = jnp.zeros(keys_all.shape, jnp.float32)
    grad_values = jnp.zeros(values.shape, jnp.float32)
    grad_pieces = []
    for offset in range(0, length_all, block_rows):
        query_rows = queries[:, offset : offset + block_rows]
        grad_rows = grad_mixed[:, offset : offset + block_rows]
        scores = jnp.einsum("dq,dk->qk", query_rows, keys_all, preferred_element_type=jnp.float32)
        scores = jnp.where(visible, scores, -1e30)
        softmax_out = jnp.exp(scores - log_sum[offset : offset + block_rows, None])
        grad_soft = jnp.einsum("dq,dk->qk", grad_rows, values, preferred_element_type=jnp.float32)
        row_dot = jnp.sum(softmax_out * grad_soft, -1, keepdims=True)
        grad_scores = (softmax_out * (grad_soft - row_dot)).astype(jnp.bfloat16)
        grad_pieces.append(
            jnp.einsum("qk,dk->dq", grad_scores, keys_all, preferred_element_type=jnp.float32)
        )
        grad_keys = grad_keys + jnp.einsum(
            "qk,dq->dk", grad_scores, query_rows, preferred_element_type=jnp.float32
        )
        grad_values = grad_values + jnp.einsum(
            "qk,dq->dk",
            softmax_out.astype(jnp.bfloat16),
            grad_rows,
            preferred_element_type=jnp.float32,
        )
    return (
        jnp.concatenate(grad_pieces, 1).astype(jnp.bfloat16),
        grad_keys.astype(jnp.bfloat16),
        grad_values.astype(jnp.bfloat16),
    )


def on_device(
    images,
    lengths,
    ln1_gain,
    ln1_bias,
    w_qkv,
    qv_bias,
    w_out,
    out_bias,
    ln2_gain,
    ln2_bias,
    w_up,
    up_bias,
    w_down,
    down_bias,
    cotangent,
):
    image_count, token_count, width_all = images.shape
    head_scale = HD ** (-0.5)
    gain_first, bias_first, qkv_full, qv_full, out_full, outb_full = (
        lax.all_gather(ln1_gain, "fsdp", axis=0, tiled=True),
        lax.all_gather(ln1_bias, "fsdp", axis=0, tiled=True),
        lax.all_gather(w_qkv, "fsdp", axis=0, tiled=True),
        lax.all_gather(qv_bias, "fsdp", axis=1, tiled=True),
        lax.all_gather(w_out, "fsdp", axis=0, tiled=True),
        lax.all_gather(out_bias, "fsdp", axis=0, tiled=True),
    )
    inputs_all = images.astype(jnp.float32)
    normed_first, norm_first_back = jax.vjp(
        normalize, inputs_all, gain_first.astype(jnp.float32), bias_first.astype(jnp.float32)
    )
    normed_attn = normed_first.astype(jnp.bfloat16)
    qkv_split = qkv_full.reshape(width_all, 3, H, HD)
    projected = jnp.einsum(
        "itd,dahe->ahiet", normed_attn, qkv_split, preferred_element_type=jnp.float32
    )
    shift_pair = qv_full.astype(jnp.float32).reshape(2, H, HD)
    queries = (projected[0] + shift_pair[0][:, None, :, None]) * head_scale
    values = projected[2] + shift_pair[1][:, None, :, None]
    stacked = jnp.stack([queries, projected[1], values]).astype(jnp.bfloat16)
    head_view = lax.all_to_all(stacked, "seq", split_axis=1, concat_axis=4, tiled=True)
    local_heads = head_view.shape[1]
    item_count = local_heads * image_count
    query_items = head_view[0].reshape(item_count, HD, -1)
    key_items = head_view[1].reshape(item_count, HD, -1)
    value_items = head_view[2].reshape(item_count, HD, -1)
    item_lengths = jnp.tile(lengths, local_heads)
    mixed_items, log_sums = lax.map(
        lambda packed: attend_item(*packed), (query_items, key_items, value_items, item_lengths)
    )
    mixed_tokens = lax.all_to_all(
        for_sending(mixed_items.reshape(local_heads, image_count, HD, -1)),
        "seq",
        split_axis=3,
        concat_axis=0,
        tiled=True,
    )
    out_split = out_full.reshape(H, HD, width_all)
    residual = (
        inputs_all
        + jnp.einsum("hiet,hed->itd", mixed_tokens, out_split, preferred_element_type=jnp.float32)
        + outb_full.astype(jnp.float32)
    )
    gain_second, bias_second, up_full, upb_full, down_full, downb_full = (
        lax.all_gather(ln2_gain, "fsdp", axis=0, tiled=True),
        lax.all_gather(ln2_bias, "fsdp", axis=0, tiled=True),
        lax.all_gather(w_up, "fsdp", axis=0, tiled=True),
        lax.all_gather(up_bias, "fsdp", axis=0, tiled=True),
        lax.all_gather(w_down, "fsdp", axis=1, tiled=True),
        lax.all_gather(down_bias, "fsdp", axis=0, tiled=True),
    )
    normed_second, norm_second_back = jax.vjp(
        normalize, residual, gain_second.astype(jnp.float32), bias_second.astype(jnp.float32)
    )
    normed_mlp = normed_second.astype(jnp.bfloat16)
    pre_act = jnp.einsum(
        "itd,df->itf", normed_mlp, up_full, preferred_element_type=jnp.float32
    ) + upb_full.astype(jnp.float32)
    activation, gelu_back = jax.vjp(gelu_tanh, pre_act)
    activation = activation.astype(jnp.bfloat16)
    output_all = (
        residual
        + jnp.einsum("itf,fd->itd", activation, down_full, preferred_element_type=jnp.float32)
        + downb_full.astype(jnp.float32)
    )
    layer_out = output_all.astype(jnp.bfloat16)
    qkv_back, out_back = (
        lax.all_gather(w_qkv, "fsdp", axis=0, tiled=True),
        lax.all_gather(w_out, "fsdp", axis=0, tiled=True),
    )
    up_back, down_back = (
        lax.all_gather(w_up, "fsdp", axis=0, tiled=True),
        lax.all_gather(w_down, "fsdp", axis=1, tiled=True),
    )
    grad_down = jnp.einsum("itf,itd->fd", activation, cotangent, preferred_element_type=jnp.float32)
    grad_downb = jnp.sum(cotangent, axis=(0, 1), dtype=jnp.float32)
    grad_act = jnp.einsum("itd,fd->itf", cotangent, down_back, preferred_element_type=jnp.float32)
    (grad_pre,) = gelu_back(grad_act)
    grad_pre = grad_pre.astype(jnp.bfloat16)
    grad_up = jnp.einsum("itd,itf->df", normed_mlp, grad_pre, preferred_element_type=jnp.float32)
    grad_upb = jnp.sum(grad_pre, axis=(0, 1), dtype=jnp.float32)
    grad_normed_mlp = jnp.einsum(
        "itf,df->itd", grad_pre, up_back, preferred_element_type=jnp.float32
    )
    grad_resid_norm, grad_gain_second, grad_bias_second = norm_second_back(grad_normed_mlp)
    grad_residual = cotangent.astype(jnp.float32) + grad_resid_norm
    grad_branch = grad_residual.astype(jnp.bfloat16)
    grad_outw = jnp.einsum(
        "hiet,itd->hed", mixed_tokens, grad_branch, preferred_element_type=jnp.float32
    ).reshape(width_all, width_all)
    grad_outb = jnp.sum(grad_branch, axis=(0, 1), dtype=jnp.float32)
    out_back_split = out_back.reshape(H, HD, width_all)
    grad_mixed = jnp.einsum(
        "itd,hed->hiet", grad_branch, out_back_split, preferred_element_type=jnp.float32
    ).astype(jnp.bfloat16)
    grad_head_view = lax.all_to_all(grad_mixed, "seq", split_axis=0, concat_axis=3, tiled=True)
    grad_items = grad_head_view.reshape(item_count, HD, -1)
    grad_q, grad_k, grad_v = lax.map(
        lambda packed: attend_back(*packed),
        (query_items, key_items, value_items, item_lengths, log_sums, grad_items),
    )
    grad_stack = jnp.stack([grad_q, grad_k, grad_v]).reshape(3, local_heads, image_count, HD, -1)
    grad_projected = lax.all_to_all(
        for_sending(grad_stack), "seq", split_axis=4, concat_axis=1, tiled=True
    ).astype(grad_stack.dtype)
    column_scales = jnp.array([head_scale, 1.0, 1.0], jnp.float32)
    grad_qkv = (
        jnp.einsum(
            "itd,ahiet->dahe", normed_attn, grad_projected, preferred_element_type=jnp.float32
        )
        * column_scales[None, :, None, None]
    ).reshape(width_all, 3 * width_all)
    shift_sums = jnp.sum(grad_projected, axis=(2, 4), dtype=jnp.float32)
    grad_qvb = jnp.stack([shift_sums[0] * head_scale, shift_sums[2]]).reshape(2, width_all)
    qkv_back_split = qkv_back.reshape(width_all, 3, H, HD)
    grad_normed_attn = head_scale * jnp.einsum(
        "hiet,dhe->itd", grad_projected[0], qkv_back_split[:, 0], preferred_element_type=jnp.float32
    )
    grad_normed_attn = grad_normed_attn + jnp.einsum(
        "ahiet,dahe->itd",
        grad_projected[1:],
        qkv_back_split[:, 1:],
        preferred_element_type=jnp.float32,
    )
    grad_input_norm, grad_gain_first, grad_bias_first = norm_first_back(grad_normed_attn)
    grad_images = (grad_residual + grad_input_norm).astype(jnp.bfloat16)
    (
        part_gone,
        part_bone,
        part_qkv,
        part_qvb,
        part_outw,
        part_outb,
        part_gtwo,
        part_btwo,
        part_up,
        part_upb,
        part_down,
        part_downb,
    ) = (
        lax.psum_scatter(
            grad_gain_first.astype(jnp.bfloat16), "fsdp", scatter_dimension=0, tiled=True
        ).astype(jnp.float32),
        lax.psum_scatter(
            grad_bias_first.astype(jnp.bfloat16), "fsdp", scatter_dimension=0, tiled=True
        ).astype(jnp.float32),
        lax.psum_scatter(
            grad_qkv.astype(jnp.bfloat16), "fsdp", scatter_dimension=0, tiled=True
        ).astype(jnp.float32),
        lax.psum_scatter(
            grad_qvb.astype(jnp.bfloat16), "fsdp", scatter_dimension=1, tiled=True
        ).astype(jnp.float32),
        lax.psum_scatter(
            grad_outw.astype(jnp.bfloat16), "fsdp", scatter_dimension=0, tiled=True
        ).astype(jnp.float32),
        lax.psum_scatter(
            grad_outb.astype(jnp.bfloat16), "fsdp", scatter_dimension=0, tiled=True
        ).astype(jnp.float32),
        lax.psum_scatter(
            grad_gain_second.astype(jnp.bfloat16), "fsdp", scatter_dimension=0, tiled=True
        ).astype(jnp.float32),
        lax.psum_scatter(
            grad_bias_second.astype(jnp.bfloat16), "fsdp", scatter_dimension=0, tiled=True
        ).astype(jnp.float32),
        lax.psum_scatter(
            grad_up.astype(jnp.bfloat16), "fsdp", scatter_dimension=0, tiled=True
        ).astype(jnp.float32),
        lax.psum_scatter(
            grad_upb.astype(jnp.bfloat16), "fsdp", scatter_dimension=0, tiled=True
        ).astype(jnp.float32),
        lax.psum_scatter(
            grad_down.astype(jnp.bfloat16), "fsdp", scatter_dimension=1, tiled=True
        ).astype(jnp.float32),
        lax.psum_scatter(
            grad_downb.astype(jnp.bfloat16), "fsdp", scatter_dimension=0, tiled=True
        ).astype(jnp.float32),
    )
    (
        final_gone,
        final_bone,
        final_qkv,
        final_qvb,
        final_outw,
        final_outb,
        final_gtwo,
        final_btwo,
        final_up,
        final_upb,
        final_down,
        final_downb,
    ) = (
        lax.psum(part_gone.astype(jnp.bfloat16), "seq").astype(jnp.float32),
        lax.psum(part_bone.astype(jnp.bfloat16), "seq").astype(jnp.float32),
        lax.psum(part_qkv.astype(jnp.bfloat16), "seq").astype(jnp.float32),
        lax.psum(part_qvb.astype(jnp.bfloat16), "seq").astype(jnp.float32),
        lax.psum(part_outw.astype(jnp.bfloat16), "seq").astype(jnp.float32),
        lax.psum(part_outb.astype(jnp.bfloat16), "seq").astype(jnp.float32),
        lax.psum(part_gtwo.astype(jnp.bfloat16), "seq").astype(jnp.float32),
        lax.psum(part_btwo.astype(jnp.bfloat16), "seq").astype(jnp.float32),
        lax.psum(part_up.astype(jnp.bfloat16), "seq").astype(jnp.float32),
        lax.psum(part_upb.astype(jnp.bfloat16), "seq").astype(jnp.float32),
        lax.psum(part_down.astype(jnp.bfloat16), "seq").astype(jnp.float32),
        lax.psum(part_downb.astype(jnp.bfloat16), "seq").astype(jnp.float32),
    )
    return (
        layer_out,
        grad_images,
        final_gone,
        final_bone,
        final_qkv,
        final_qvb,
        final_outw,
        final_outb,
        final_gtwo,
        final_btwo,
        final_up,
        final_upb,
        final_down,
        final_downb,
    )


def solution(mesh):
    placed = (
        P("fsdp", "seq", None),
        P("fsdp"),
        P("fsdp"),
        P("fsdp"),
        P("fsdp", None),
        P(None, "fsdp"),
        P("fsdp", None),
        P("fsdp"),
        P("fsdp"),
        P("fsdp"),
        P("fsdp", None),
        P("fsdp"),
        P(None, "fsdp"),
        P("fsdp"),
        P("fsdp", "seq", None),
    )
    return jax.shard_map(
        on_device,
        mesh=mesh,
        in_specs=placed,
        out_specs=(
            P("fsdp", "seq", None),
            P("fsdp", "seq", None),
            P("fsdp"),
            P("fsdp"),
            P("fsdp", None),
            P(None, "fsdp"),
            P("fsdp", None),
            P("fsdp"),
            P("fsdp"),
            P("fsdp"),
            P("fsdp", None),
            P("fsdp"),
            P(None, "fsdp"),
            P("fsdp"),
        ),
        check_vma=False,
    )
```

profile of v0, /device:TPU:0, one launch (start us, length us, event | category | flops | bytes accessed | tf_op | source)
XLA Modules:
  0.0 1667.9 jit_solution(1936642603031009704)
XLA Ops:
  13.0 18.5 %all-reduce.17 = (bf16[1152]{0:T(1024)(128)(2,1)S(1)}, bf16[1152]{0:T(1024)(128)(2,1)S(1)}, bf16[1152]{0:T(1024)(128)(2,1)S(1)}, bf16[1152]{0:T(1024)(128)(2,1)S...) all-reduce(bf16[1152]{0:T(1024)(128)(2,1)S(1)} %dynamic-update-slic, ...), channel_id=1, replica_groups=mesh['fsdp'=4,'seq'=8] {'fsdp'}, use_global_device_ids=true, to_apply=%add.1 | all-reduce | flops 10064 | bytes 40256
  33.3 7.5 all-gather
  41.1 55.8 %all-gather.6.cloned.1.call-done = bf16[1152,3456]{1,0:T(8,128)(2,1)} async-done(((bf16[288,3456]{1,0:T(8,128)(2,1)}), bf16[1152,3456]{1,0:T(8,128)(2,1)}) %all-gather.6.cloned.1.call-update) | async-done | bytes 7962640 | tf_op jit(solution)/shard_map/all_gather | solution.py:113
  96.9 11.5 copy.97
  108.5 12.5 convolution_bitcast_fusion.3
  123.5 4.8 copy.99
  128.3 5.0 all-to-all-start
  133.9 155.1 %all-to-all-done = bf16[3,16,8,72,128]{4,3,0,2,1:T(8,128)(2,1)} async-done(((bf16[3,16,8,72,128]{4,3,0,2,1:T(8,128)(2,1)}), bf16[3,16,8,72,128]{4,3,0,2,1:T(8,128)(2,1)}, u32[]{:S(2)}, u32[]{:S(2)}) %all-to-all-start) | async-done | bytes 7077920 | tf_op jit(solution)/shard_map/all_to_all | solution.py:131
  289.0 7.7 fusion.114
  299.6 5.0 reshape_squeeze.10
  304.6 4.6 copy.102
  309.2 4.9 reshape_squeeze.11
  314.1 4.6 copy.100
  318.7 4.9 reshape_squeeze.9
  325.3 180.0 %while.26 = (s32[]{:T(128)}, bf16[16,72,1024]{2,1,0:T(8,128)(2,1)}, f32[16,1024]{1,0:T(8,128)}, bf16[16,72,1024]{2,1,0:T(8,128)(2,1)}, s32[16]{0:T(128)S(1)}, /*...) while((s32[]{:T(128)}, bf16[16,72,1024]{2,1,0:T(8,128)(2,1)}, ...), condition=%wide.region_5.6_spmd, body=%wide.region_2.5_spmd.sunk | while | flops 311500800 | bytes 29997196 | solution.py:138
  332.6 4.0 fusion.152
  343.8 4.0 fusion.152
  355.1 4.0 fusion.152
  366.3 4.0 fusion.152
  377.6 4.0 fusion.152
  388.8 4.0 fusion.152
  400.1 4.0 fusion.152
  411.3 4.0 fusion.152
  422.6 4.0 fusion.152
  433.8 4.0 fusion.152
  445.1 4.0 fusion.152
  456.3 4.0 fusion.152
  467.6 4.0 fusion.152
  478.8 4.0 fusion.152
  490.1 4.0 fusion.152
  505.4 6.3 copy.103
  511.7 4.5 all-to-all-start.1
  516.7 93.5 %all-to-all-done.1 = bf16[2,8,72,1024]{2,1,0,3:T(8,128)(2,1)} async-done(((bf16[2,8,72,1024]{2,1,0,3:T(8,128)(2,1)}), bf16[2,8,72,1024]{2,1,0,3:T(8,128)(2,1)}, u32[]{:S(2)}, u32[]{:S(2)}) %all-to-all-start.1) | async-done | bytes 2359328 | tf_op jit(solution)/shard_map/all_to_all | solution.py:141
  610.2 6.3 copy.105
  616.5 6.5 fusion.116
  625.9 24.8 %multiply_convert_fusion.1 = (bf16[8,128,4304]{1,2,0:T(8,128)(2,1)}, f32[8,128,4304]{1,2,0:T(8,128)}) fusion(f32[4304]{0:T(1024)S(1)} %convert_element_type.186, bf16[1152,4304]{1,0:T(8,128)(2,1)} %all-gather.10.cloned.1.call-done, f32[8,128,1152]{2,1,0:T(8,128)} %copy-done.5, f32[1152]{0:T(1024)S(1)} %convert_element_type.184, ...), kind=kOutput, calls=%fused_computation.72 | convolution fusion | flops 10204381184 | bytes 41113408 | tf_op jit(solution)/shard_map/itd,df->itf/dot_general | solution.py:166
  650.7 32.5 %fusion.117 = (bf16[4304]{0:T(1024)(128)(2,1)}, bf16[8,128,4304]{1,2,0:T(8,128)(2,1)}) fusion(f32[8,128,4304]{1,2,0:T(8,128)} %get-tuple-element.199, f32[4304]{0:T(1024)S(1)} %convert_element_type.186, bf16[8,128,1152]{2,1,0:T(8,128)(2,1)} %param.34, bf16[4304,1152]{0,1:T(8,128)(2,1)} %all-gather.12.cloned.1.call-done), kind=kOutput, calls=%fused_computation.155 | convolution fusion | flops 10251366400 | bytes 38745312 | tf_op jit(solution)/shard_map/itd,fd->itf/dot_general | solution.py:187
  683.2 20.6 %multiply_reduce_fusion.1 = (bf16[1152]{0:T(1024)(128)(2,1)}, f32[8,128]{1,0:T(8,128)S(1)}, bf16[1152]{0:T(1024)(128)(2,1)}, f32[8,128,1152]{2,1,0:T(8,128)}) fusion(f32[8,128,1152]{2,1,0:T(8,128)S(1)} %bitcast.254, f32[8,128]{1,0:T(8,128)S(1)} %fusion.109, f32[8,128]{1,0:T(8,128)S(1)} %broadcast_multiply_fusion, f32[1152]{0:T(1024)S(1)} %convert_element_type.183, ...), kind=kOutput, calls=%fused_computation.117 | convolution fusion | flops 10163844096 | bytes 28189696 | tf_op jit(solution)/shard_map/itf,df->itd/dot_general | solution.py:192
  710.9 4.4 fusion.71
  715.4 19.1 %fusion.54 = bf16[1152,4304]{1,0:T(8,128)(2,1)} fusion(bf16[8,128,4304]{1,2,0:T(8,128)(2,1)} %get-tuple-element.203, f32[8,128,1152]{2,1,0:T(8,128)} %copy-done.5, f32[1152]{0:T(1024)S(1)} %convert_element_type.184, f32[1152]{0:T(1024)S(1)} %convert_element_type.183, f32[8,128]{1,0:T(8,128)S(1)} %fusion.109, f32[8,128]{1,0:T(8,128)S(1)} %broadcast_multiply_fusion), kind=kOutput, calls=%fused_computation.63 | convolution fusion | flops 10165266432 | bytes 23467008 | tf_op jit(solution)/shard_map/itd,itf->df/dot_general | solution.py:190
  736.3 4.8 convert_bitcast_fusion
  742.9 4.4 all-to-all-start.2
  747.3 16.5 fusion.55
  764.1 37.8 %all-to-all-done.2 = bf16[16,8,72,128]{3,2,1,0:T(8,128)(2,1)} async-done(((bf16[16,8,72,128]{3,2,1,0:T(8,128)(2,1)}), bf16[16,8,72,128]{3,2,1,0:T(8,128)(2,1)}, u32[]{:S(2)}, u32[]{:S(2)}) %all-to-all-start.2) | async-done | bytes 2359328 | tf_op jit(solution)/shard_map/all_to_all | solution.py:206
  811.2 220.9 %while.27 = (s32[]{:T(128)}, bf16[16,72,1024]{2,1,0:T(8,128)(2,1)S(1)}, bf16[16,72,1024]{2,1,0:T(8,128)(2,1)}, bf16[16,72,1024]{2,1,0:T(8,128)(2,1)}, bf16[16,72...) while((s32[]{:T(128)}, ...), condition=%wide.region_12.13_spmd, body=%wide.region_10.12_spmd.sunk | while | flops 767778816 | bytes 32969856 | solution.py:208
  1032.1 4.9 copy.108
  1037.0 6.4 copy.109
  1043.4 6.3 copy.110
  1049.7 6.9 pad_maximum_fusion
  1056.7 277.4 %all_to_all.66 = bf16[3,2,8,72,1024]{3,2,1,0,4:T(8,128)(2,1)} all-to-all(bf16[3,2,8,72,1024]{3,2,1,0,4:T(8,128)(2,1)S(1)} %pad_maximum_fusion), channel_id=1, replica_groups=mesh['fsdp'=4,'seq'=8] {'seq'}, dimensions={4} | all-to-all | bytes 14155776 | tf_op jit(solution)/shard_map/all_to_all | solution.py:213
  1334.1 15.4 copy.114
  1349.5 13.9 fusion.63
  1363.4 11.6 copy.115
  1376.8 13.2 copy.133
  1390.1 4.5 convert_reduce_fusion
  1405.6 5.8 fusion.98
  1411.4 8.9 fusion.110
  1424.5 17.1 %all-reduce.16 = (bf16[1152]{0:T(1024)(128)(2,1)S(1)}, bf16[1152]{0:T(1024)(128)(2,1)S(1)}, bf16[1152]{0:T(1024)(128)(2,1)S(1)}, bf16[1152]{0:T(1024)(128)(2,1)S...) all-reduce(bf16[1152]{0:T(1024)(128)(2,1)S(1)} %dynamic-update-slic, ...), channel_id=1, replica_groups=mesh['fsdp'=4,'seq'=8] {'fsdp'}, use_global_device_ids=true, to_apply=%add.6 | all-reduce | flops 12368 | bytes 49472
  1442.2 15.3 reduce-scatter.8.cloned.1.call-done
  1457.5 6.5 add_convert_fusion
  1464.1 19.0 %fusion.94 = bf16[8,128,1152]{2,1,0:T(8,128)(2,1)} fusion(f32[8,128,1152]{2,1,0:T(8,128)} %copy-done.5, bf16[8,128,4304]{1,2,0:T(8,128)(2,1)} %get-tuple-element.198, bf16[4304,1152]{0,1:T(8,128)(2,1)} %all-gather.12.cloned.1.call-done, f32[1152]{0:T(1024)S(1)} %convert_element_type.188), kind=kOutput, calls=%fused_computation.123 | convolution fusion | flops 10157948928 | bytes 25813504 | tf_op jit(solution)/shard_map/itf,fd->itd/dot_general | solution.py:173
  1486.2 29.3 %all-reduce.14 = (bf16[288]{0:T(512)(128)(2,1)S(1)}, bf16[288]{0:T(512)(128)(2,1)S(1)}, bf16[2,288]{1,0:T(2,128)(2,1)S(1)}, bf16[288]{0:T(512)(128)(2,1)S(1)}, b...) all-reduce(bf16[288]{0:T(512)(128)(2,1)S(1)} %dynamic-slice.8, ...), channel_id=1, replica_groups=mesh['fsdp'=4,'seq'=8] {'seq'}, use_global_device_ids=true, to_apply=%region_17.18 | all-reduce | flops 3380 | bytes 13520 | tf_op jit(solution)/shard_map/psum | solution.py:302
  1520.2 130.0 %all-reduce.20.cloned.1.call-done = (bf16[288,3456]{1,0:T(8,128)(2,1)}, bf16[288,1152]{1,0:T(8,128)(2,1)}, bf16[288,4304]{1,0:T(8,128)(2,1)}, bf16[4304,288]{0,1:T(8,128)(2,1)}) async-done(((bf16[288,3456]{1,0:T(8,128)(2,1)}, bf16[288,1152]{1,0:T(8,128)(2,1)}, bf16[288,4304]{1,0:T(8,128)(2,1)}, bf16[4304,288]{0,1:T(8,128)(2,1)}), (bf16[288,3456]{1,0:T(8,128)(2,1)}, bf16[288,1152]{1,0:T(8,128)(2,1)}, ...) | async-done | bytes 7612432 | tf_op jit(solution)/shard_map/psum | solution.py:304
  1650.2 4.5 convert_element_type.213
  (486 shorter events, 406.9 us)
Async XLA Ops:
  7.2 2.3 copy-start.33
  7.2 4.2 copy-start.35
  7.2 4.5 copy-start.36
  7.2 4.7 copy-start.37
  7.2 5.0 copy-start.38
  7.2 5.2 copy-start.39
  7.2 5.5 copy-start.32
  7.3 24.2 %copy-start.2 = (bf16[8,128,1152]{2,1,0:T(8,128)(2,1)S(1)}, bf16[8,128,1152]{2,1,0:T(8,128)(2,1)}, u32[]{:S(2)}) copy-start(bf16[8,128,1152]{2,1,0:T(8,128)(2,1)} %param.20) | copy-start | bytes 7077892
  7.3 26.0 %copy-start.34 = (bf16[2,288]{1,0:T(2,128)(2,1)S(1)}, bf16[2,288]{1,0:T(2,128)(2,1)}, u32[]{:S(2)}) copy-start(bf16[2,288]{1,0:T(2,128)(2,1)} %param.25) | copy-start | bytes 3460
  7.3 89.6 %all-gather.6.cloned.1.call-start = ((), (), s32[]{:S(2)}) async-start(), calls=%async_computation.9 | async-start | bytes 9953280 | tf_op jit(solution)/shard_map/all_gather | solution.py:113
  8.0 608.5 %all-gather.8.cloned.1.call-start = ((), (), s32[]{:S(2)}) async-start(), calls=%async_computation.10 | async-start | bytes 3317760 | tf_op jit(solution)/shard_map/all_gather | solution.py:115
  8.8 617.1 %all-gather.10.cloned.1.call-start = ((), (), s32[]{:S(2)}) async-start(), calls=%async_computation.11 | async-start | bytes 12533760 | tf_op jit(solution)/shard_map/all_gather | solution.py:157
  31.5 77.0 %copy-start.15 = (f32[1152]{0:T(1024)}, f32[1152]{0:T(1024)S(1)}, u32[]{:S(2)}) copy-start(f32[1152]{0:T(1024)S(1)} %convert_element_type.178) | copy-start | bytes 13828
  31.5 77.0 %copy-start.28 = (f32[1152]{0:T(1024)}, f32[1152]{0:T(1024)S(1)}, u32[]{:S(2)}) copy-start(f32[1152]{0:T(1024)S(1)} %convert_element_type.179) | copy-start | bytes 13828
  31.9 76.6 %copy-start.17 = (f32[8,128]{1,0:T(8,128)}, f32[8,128]{1,0:T(8,128)S(1)}, u32[]{:S(2)}) copy-start(f32[8,128]{1,0:T(8,128)S(1)} %broadcast_multiply_fusion.1) | copy-start | bytes 12292
  32.7 75.8 %copy-start.21 = (f32[8,128]{1,0:T(8,128)}, f32[8,128]{1,0:T(8,128)S(1)}, u32[]{:S(2)}) copy-start(f32[8,128]{1,0:T(8,128)S(1)} %fusion.108) | copy-start | bytes 12292
  128.3 5.6 copy-start.41
  128.3 160.7 %all-to-all-start = ((bf16[3,16,8,72,128]{4,3,0,2,1:T(8,128)(2,1)}), bf16[3,16,8,72,128]{4,3,0,2,1:T(8,128)(2,1)}, u32[]{:S(2)}, u32[]{:S(2)}) async-start(bf16[3,16,8,72,128]{4,3,0,2,1:T(8,128)(2,1)} %copy.99), calls=%async_computation | async-start | bytes 14155776 | tf_op jit(solution)/shard_map/all_to_all | solution.py:131
  133.2 517.4 %all-gather.12.cloned.1.call-start = ((), (), s32[]{:S(2)}) async-start(), calls=%async_computation.12 | async-start | bytes 12533760 | tf_op jit(solution)/shard_map/all_gather | solution.py:159
  328.3 2.0 copy-start
  350.8 2.0 copy-start
  362.1 2.0 copy-start
  373.3 2.0 copy-start
  384.6 2.0 copy-start
  407.1 2.0 copy-start
  418.4 2.0 copy-start
  505.4 6.3 copy-start.42
  511.7 98.5 %all-to-all-start.1 = ((bf16[2,8,72,1024]{2,1,0,3:T(8,128)(2,1)}), bf16[2,8,72,1024]{2,1,0,3:T(8,128)(2,1)}, u32[]{:S(2)}, u32[]{:S(2)}) async-start(bf16[2,8,72,1024]{2,1,0,3:T(8,128)(2,1)} %bitcast.255), calls=%async_computation.1 | async-start | bytes 8388608 | tf_op jit(solution)/shard_map/all_to_all | solution.py:141
  516.2 926.0 %reduce-scatter.10.cloned.1.call-start = ((), (), s32[]{:S(2)}) async-start(), calls=%async_computation.14 | async-start | bytes 3317760 | tf_op jit(solution)/shard_map/reduce_scatter | solution.py:263
  623.1 2.2 copy-start.5
  625.9 57.3 %slice-start = ((s8[4718592]{0:T(1024)(128)(4,1)}), s8[524288]{0:T(1024)(128)(4,1)S(1)}, s32[]{:S(2)}) async-start(s8[4718592]{0:T(1024)(128)(4,1)} %bitcast.253), calls=%async_computation.19 | async-start | bytes 1048576
  650.7 32.5 %slice-start.1 = ((s8[4718592]{0:T(1024)(128)(4,1)}), s8[4194304]{0:T(1024)(128)(4,1)S(1)}, s32[]{:S(2)}) async-start(s8[4718592]{0:T(1024)(128)(4,1)} %bitcast.253), calls=%async_computation.20 | async-start | bytes 8388608
  703.8 3.3 copy-start.7
  707.1 2.4 copy-start.4
  707.1 2.4 copy-start.19
  707.1 3.8 copy-start.9
  715.4 726.9 %reduce-scatter.12.cloned.1.call-start = ((), (), s32[]{:S(2)}) async-start(), calls=%async_computation.15 | async-start | bytes 12533760 | tf_op jit(solution)/shard_map/reduce_scatter | solution.py:275
  741.1 6.2 copy-start.8
  742.9 59.0 %all-to-all-start.2 = ((bf16[16,8,72,128]{3,2,1,0:T(8,128)(2,1)}), bf16[16,8,72,128]{3,2,1,0:T(8,128)(2,1)}, u32[]{:S(2)}, u32[]{:S(2)}) async-start(bf16[16,8,72,128]{3,2,1,0:T(8,128)(2,1)} %copy.106), calls=%async_computation.2 | async-start | bytes 4718592 | tf_op jit(solution)/shard_map/all_to_all | solution.py:206
  747.2 695.0 %reduce-scatter.14.cloned.1.call-start = ((), (), s32[]{:S(2)}) async-start(), calls=%async_computation.16 | async-start | bytes 12533760 | tf_op jit(solution)/shard_map/reduce_scatter | solution.py:281
  763.8 693.7 %reduce-scatter.8.cloned.1.call-start = ((), (), s32[]{:S(2)}) async-start(), calls=%async_computation.13 | async-start | bytes 9953280 | tf_op jit(solution)/shard_map/reduce_scatter | solution.py:257
  807.5 3.7 copy-start.43
  1334.0 15.4 copy-start.3
  1334.0 15.4 copy-start.16
  1334.0 15.4 copy-start.18
  1334.0 15.4 copy-start.22
  1334.0 15.4 copy-start.29
  1334.1 15.4 copy-start.44
  1375.0 110.2 %reduce-scatter.16.cloned.1.call-start = ((), (), s32[]{:S(2)}) async-start(), calls=%async_computation.17 | async-start | bytes 368640
  1390.1 5.6 copy-start.1
  1401.2 3.3 copy-start.6
  1404.5 6.8 slice-start.2
  1405.6 5.8 slice-start.3
  1411.4 8.9 copy-start.24
  1420.3 4.1 copy-start.25
  1420.3 4.1 copy-start.26
  1420.3 4.1 copy-start.27
  1420.3 4.2 copy-start.30
  1420.3 4.2 copy-start.31
  1420.4 229.8 %all-reduce.20.cloned.1.call-start = ((), (), s32[]{:S(2)}) async-start(), calls=%async_computation.18 | async-start | bytes 15335424 | tf_op jit(solution)/shard_map/psum | solution.py:304
  1424.4 33.1 %copy-start.20 = (f32[8,128]{1,0:T(8,128)S(1)}, f32[8,128]{1,0:T(8,128)}, u32[]{:S(2)}) copy-start(f32[8,128]{1,0:T(8,128)} %copy-done.19) | copy-start | bytes 12292
  1650.2 4.5 copy-start.11
  1654.6 2.6 copy-start.13
  1657.3 2.2 copy-start.14
  (13 other events, 23.5 us)
Sparse Core Ops, SparseCore 0:
  9.9 86.9 all-gather.5
  98.8 39.7 all-gather.7
  140.4 101.0 all-gather.9
  243.3 101.0 all-gather.11
  715.5 38.3 reduce-scatter.9
  756.9 99.6 reduce-scatter.11
  859.8 99.6 reduce-scatter.13
  1375.1 82.3 reduce-scatter.7
  1460.8 24.3 reduce-scatter.15
  1487.7 162.3 all-reduce.19
where the time goes:
time: 1680 us; the launch traced here: 1670 us
  waiting for transfers between devices  492 us (29%)
  matrix products  447 us (27%)
  blocking collectives  350 us (21%)
  local copies, waits for them, and re-layouts  242 us (14%)
  other arithmetic  102 us (6%)
  between operations  18 us (1%)
    all_to_all x1, blocking collectives, on_device(): lax.all_to_all(for_sending(grad_stack), 'seq', split_axis=4, concat_axis=...  277 us
    all_to_all x1, waiting for transfers between devices, on_device(): lax.all_to_all(stacked, 'seq', split_axis=1, concat_axis=4, tiled=True)  155 us
    psum x1, waiting for transfers between devices, on_device(): lax.psum(part_qkv.astype(jnp.bfloat16), 'seq').astype(jnp.float32)  130 us
    all_to_all x1, waiting for transfers between devices, on_device(): lax.all_to_all(for_sending(mixed_items.reshape(local_heads, image_count,...  93.5 us
    dot_general x16, matrix products, attend_item(): jnp.einsum('qk,dk->dq', softmax_low, values, preferred_element_type=jnp.f...  64.5 us
    all_gather x1, waiting for transfers between devices, on_device(): lax.all_gather(w_qkv, 'fsdp', axis=0, tiled=True)  55.8 us
    dot_general x16, matrix products, attend_back(): jnp.einsum('qk,dq->dk', softmax_out.astype(jnp.bfloat16), grad_rows, pref...  42.4 us
    all_to_all x1, waiting for transfers between devices, on_device(): lax.all_to_all(grad_mixed, 'seq', split_axis=0, concat_axis=3, tiled=True)  37.8 us
  transfers between devices with their start and end apart: 13, of which 7 were waited for; matrix products, arithmetic and copies ran while one was open for 41% of the time, Pallas kernels for 0%

commit v1 on v0

--- a/solution.py
+++ b/solution.py
@@ -7,6 +7,24 @@
 HD = 72
 epsilon = 1e-06
 wide_block = 1024
+
+
+def gather_around(array, axis, dim):
+    ways, here, hop = (lax.axis_size(axis), lax.axis_index(axis), array.shape[dim])
+    shape = [n * ways if d == dim else n for d, n in enumerate(array.shape)]
+    full = lax.dynamic_update_slice_in_dim(
+        jnp.zeros(shape, array.dtype), array, here * hop, axis=dim
+    )
+    going_up = going_down = array
+    for far in range(1, ways // 2 + 1):
+        going_up = lax.ppermute(going_up, axis, [(d, (d + 1) % ways) for d in range(ways)])
+        full = lax.dynamic_update_slice_in_dim(full, going_up, (here - far) % ways * hop, axis=dim)
+        if 2 * far < ways:
+            going_down = lax.ppermute(going_down, axis, [(d, (d - 1) % ways) for d in range(ways)])
+            full = lax.dynamic_update_slice_in_dim(
+                full, going_down, (here + far) % ways * hop, axis=dim
+            )
+    return full
 
 
 def for_sending(shard):
@@ -110,7 +128,7 @@
     gain_first, bias_first, qkv_full, qv_full, out_full, outb_full = (
         lax.all_gather(ln1_gain, "fsdp", axis=0, tiled=True),
         lax.all_gather(ln1_bias, "fsdp", axis=0, tiled=True),
-        lax.all_gather(w_qkv, "fsdp", axis=0, tiled=True),
+        gather_around(w_qkv, "fsdp", 0),
         lax.all_gather(qv_bias, "fsdp", axis=1, tiled=True),
         lax.all_gather(w_out, "fsdp", axis=0, tiled=True),
         lax.all_gather(out_bias, "fsdp", axis=0, tiled=True),

time: 1680 us -> 1940 us (1.15)
  blocking collectives: 350 us -> 484 us
  local copies, waits for them, and re-layouts: 242 us -> 368 us
    unnamed x2, blocking collectives: 35.6 us -> 169 us
    dynamic_update_slice x0 -> x4, local copies, waits for them, and re-layouts: none -> 107 us  [the longest x2 54.6 us: gather_around(): lax.dynamic_update_slice_in_dim(full, going_up, (here - far) % ways * hop...]
    ppermute x0 -> x3, waiting for transfers between devices: none -> 65.8 us  [the longest x2 65.8 us: gather_around(): lax.ppermute(going_up, axis, [(d, (d + 1) % ways) for d in range(ways)])]
    all_gather x1, waiting for transfers between devices: 55.8 us -> 0.01 us  [on_device(): lax.all_gather(w_qkv, 'fsdp', axis=0, tiled=True)]
  transfers between devices with their start and end apart: 13 -> 16, of which waited for: 7 -> 7; matrix products, arithmetic and copies ran while one was open for 41% -> 45% of each run, Pallas kernels for 0% -> 0%
where the time goes in v1:
time: 1940 us; the launch traced here: 1930 us
  waiting for transfers between devices  489 us (25%)
  blocking collectives  484 us (25%)
  matrix products  447 us (23%)
  local copies, waits for them, and re-layouts  368 us (19%)
  other arithmetic  102 us (5%)
  starting transfers between devices  21.1 us (1%)
    all_to_all x1, blocking collectives, on_device(): lax.all_to_all(for_sending(grad_stack), 'seq', split_axis=4, concat_axis=...  277 us
    unnamed x2, blocking collectives  169 us
    all_to_all x1, waiting for transfers between devices, on_device(): lax.all_to_all(stacked, 'seq', split_axis=1, concat_axis=4, tiled=True)  155 us
    psum x1, waiting for transfers between devices, on_device(): lax.psum(part_qkv.astype(jnp.bfloat16), 'seq').astype(jnp.float32)  130 us
    all_to_all x1, waiting for transfers between devices, on_device(): lax.all_to_all(for_sending(mixed_items.reshape(local_heads, image_count,...  92.8 us
    ppermute x2, waiting for transfers between devices, gather_around(): lax.ppermute(going_up, axis, [(d, (d + 1) % ways) for d in range(ways)])  65.8 us
    dot_general x16, matrix products, attend_item(): jnp.einsum('qk,dk->dq', softmax_low, values, preferred_element_type=jnp.f...  64.5 us
    dynamic_update_slice x2, local copies, waits for them, and re-layouts, gather_around(): lax.dynamic_update_slice_in_dim(full, going_up, (here - far) % ways * hop...  54.6 us
  transfers between devices with their start and end apart: 16, of which 7 were waited for; matrix products, arithmetic and copies ran while one was open for 45% of the time, Pallas kernels for 0%

profile of v1, /device:TPU:0, one launch (start us, length us, event | category | flops | bytes accessed | tf_op | source)
XLA Modules:
  0.0 1929.2 jit_solution(9431340794616135048)
XLA Ops:
  12.1 65.8 %collective-permute-done = bf16[288,3456]{1,0:T(8,128)(2,1)} collective-permute-done((bf16[288,3456]{1,0:T(8,128)(2,1)}, bf16[288,3456]{1,0:T(8,128)(2,1)}, u32[]{:S(2)}, u32[]{:S(2)}) %collective-permute-start) | collective-permute-done | bytes 1990688 | tf_op jit(solution)/shard_map/ppermute | solution.py:20
  79.0 4.2 copy.113
  86.7 150.4 %all-reduce.17 = (bf16[1152]{0:T(1024)(128)(2,1)S(1)}, bf16[1152]{0:T(1024)(128)(2,1)S(1)}, bf16[1152]{0:T(1024)(128)(2,1)S(1)}, bf16[1152]{0:T(1024)(128)(2,1)S...) all-reduce(bf16[1152]{0:T(1024)(128)(2,1)S(1)} %dynamic-update-slic, ...), channel_id=1, replica_groups=mesh['fsdp'=4,'seq'=8] {'fsdp'}, use_global_device_ids=true, to_apply=%add.1 | all-reduce | flops 10064 | bytes 40256
  237.1 8.2 all-gather
  249.3 24.5 %dynamic_update_slice.29 = bf16[1152,3456]{0,1:T(8,128)(2,1)} dynamic-update-slice(bf16[1152,3456]{0,1:T(8,128)(2,1)} %broadcast_in_dim.72, bf16[288,3456]{0,1:T(8,128)(2,1)} %copy.113, s32[]{:T(128)S(6)} %select_n.34, s32[]{:T(128)} %copy.201) | dynamic-update-slice | bytes 3981316 | tf_op jit(solution)/shard_map/dynamic_update_slice | solution.py:15
  275.6 4.2 copy.114
  279.8 27.0 %dynamic_update_slice.30 = bf16[1152,3456]{0,1:T(8,128)(2,1)} dynamic-update-slice(bf16[1152,3456]{0,1:T(8,128)(2,1)} %dynamic_update_slice.29, bf16[288,3456]{0,1:T(8,128)(2,1)} %copy.114, s32[]{:T(128)S(6)} %select_n.36, s32[]{:T(128)} %copy.201) | dynamic-update-slice | bytes 3981316 | tf_op jit(solution)/shard_map/dynamic_update_slice | solution.py:21
  306.8 4.2 copy.115
  311.0 27.8 %dynamic_update_slice.31 = bf16[1152,3456]{0,1:T(8,128)(2,1)} dynamic-update-slice(bf16[1152,3456]{0,1:T(8,128)(2,1)} %dynamic_update_slice.30, bf16[288,3456]{0,1:T(8,128)(2,1)} %copy.115, s32[]{:T(128)S(6)} %select_n.38, s32[]{:T(128)} %copy.201) | dynamic-update-slice | bytes 3981316 | tf_op jit(solution)/shard_map/dynamic_update_slice | solution.py:24
  338.8 4.2 copy.116
  343.0 27.6 %dynamic_update_slice.32 = bf16[1152,3456]{0,1:T(8,128)(2,1)} dynamic-update-slice(bf16[1152,3456]{0,1:T(8,128)(2,1)} %dynamic_update_slice.31, bf16[288,3456]{0,1:T(8,128)(2,1)} %copy.116, s32[]{:T(128)S(6)} %select_n.40, s32[]{:T(128)} %copy.201) | dynamic-update-slice | bytes 3981316 | tf_op jit(solution)/shard_map/dynamic_update_slice | solution.py:21
  370.6 12.4 convolution_bitcast_fusion.3
  385.6 4.2 copy.118
  389.7 5.3 all-to-all-start
  395.9 155.0 %all-to-all-done = bf16[3,16,8,72,128]{4,3,2,0,1:T(8,128)(2,1)} async-done(((bf16[3,16,8,72,128]{4,3,2,0,1:T(8,128)(2,1)}), bf16[3,16,8,72,128]{4,3,2,0,1:T(8,128)(2,1)}, u32[]{:S(2)}, u32[]{:S(2)}) %all-to-all-start) | async-done | bytes 7077920 | tf_op jit(solution)/shard_map/all_to_all | solution.py:149
  550.9 6.7 fusion.113
  560.5 5.0 reshape_squeeze.10
  565.5 4.6 copy.121
  570.1 4.9 reshape_squeeze.11
  575.0 4.6 copy.119
  579.6 4.9 reshape_squeeze.9
  586.2 180.0 %while.26 = (s32[]{:T(128)}, bf16[16,72,1024]{2,1,0:T(8,128)(2,1)}, f32[16,1024]{1,0:T(8,128)}, bf16[16,72,1024]{2,1,0:T(8,128)(2,1)}, s32[16]{0:T(128)S(1)}, /*...) while((s32[]{:T(128)}, bf16[16,72,1024]{2,1,0:T(8,128)(2,1)}, ...), condition=%wide.region_5.6_spmd, body=%wide.region_2.5_spmd.sunk | while | flops 311500800 | bytes 29997196 | solution.py:156
  593.5 4.0 fusion.151
  604.7 4.0 fusion.151
  616.0 4.0 fusion.151
  627.2 4.0 fusion.151
  638.5 4.0 fusion.151
  649.7 4.0 fusion.151
  661.0 4.0 fusion.151
  672.2 4.0 fusion.151
  766.2 6.3 copy.122
  772.6 4.6 all-to-all-start.1
  778.3 92.8 %all-to-all-done.1 = bf16[2,8,72,1024]{2,1,0,3:T(8,128)(2,1)} async-done(((bf16[2,8,72,1024]{2,1,0,3:T(8,128)(2,1)}), bf16[2,8,72,1024]{2,1,0,3:T(8,128)(2,1)}, u32[]{:S(2)}, u32[]{:S(2)}) %all-to-all-start.1) | async-done | bytes 2359328 | tf_op jit(solution)/shard_map/all_to_all | solution.py:159
  871.1 6.3 copy.124
  877.4 6.5 fusion.115
  886.8 24.8 %multiply_convert_fusion.1 = (bf16[8,128,4304]{1,2,0:T(8,128)(2,1)}, f32[8,128,4304]{1,2,0:T(8,128)}) fusion(f32[4304]{0:T(1024)S(1)} %convert_element_type.186, bf16[1152,4304]{1,0:T(8,128)(2,1)} %all-gather.8.cloned.1.call-done, f32[8,128,1152]{2,1,0:T(8,128)} %copy-done.5, f32[1152]{0:T(1024)S(1)} %convert_element_type.184, ...), kind=kOutput, calls=%fused_computation.72 | convolution fusion | flops 10204381184 | bytes 41113408 | tf_op jit(solution)/shard_map/itd,df->itf/dot_general | solution.py:184
  911.6 32.5 %fusion.116 = (bf16[4304]{0:T(1024)(128)(2,1)}, bf16[8,128,4304]{1,2,0:T(8,128)(2,1)}) fusion(f32[8,128,4304]{1,2,0:T(8,128)} %get-tuple-element.199, f32[4304]{0:T(1024)S(1)} %convert_element_type.186, bf16[8,128,1152]{2,1,0:T(8,128)(2,1)} %param.34, bf16[4304,1152]{0,1:T(8,128)(2,1)} %all-gather.10.cloned.1.call-done), kind=kOutput, calls=%fused_computation.154 | convolution fusion | flops 10251366400 | bytes 38745312 | tf_op jit(solution)/shard_map/itd,fd->itf/dot_general | solution.py:205
  944.1 20.6 %multiply_reduce_fusion.1 = (bf16[1152]{0:T(1024)(128)(2,1)}, f32[8,128]{1,0:T(8,128)S(1)}, bf16[1152]{0:T(1024)(128)(2,1)}, f32[8,128,1152]{2,1,0:T(8,128)}) fusion(f32[8,128,1152]{2,1,0:T(8,128)S(1)} %bitcast.254, f32[8,128]{1,0:T(8,128)S(1)} %fusion.108, f32[8,128]{1,0:T(8,128)S(1)} %broadcast_multiply_fusion, f32[1152]{0:T(1024)S(1)} %convert_element_type.183, ...), kind=kOutput, calls=%fused_computation.117 | convolution fusion | flops 10163844096 | bytes 28189696 | tf_op jit(solution)/shard_map/itf,df->itd/dot_general | solution.py:210
  971.8 4.4 fusion.71
  976.3 19.1 fusion.54
  997.1 4.8 convert_bitcast_fusion
  1003.7 4.4 all-to-all-start.2
  1008.1 16.6 fusion.55
  1025.0 37.7 %all-to-all-done.2 = bf16[16,8,72,128]{3,2,1,0:T(8,128)(2,1)} async-done(((bf16[16,8,72,128]{3,2,1,0:T(8,128)(2,1)}), bf16[16,8,72,128]{3,2,1,0:T(8,128)(2,1)}, u32[]{:S(2)}, u32[]{:S(2)}) %all-to-all-start.2) | async-done | bytes 2359328 | tf_op jit(solution)/shard_map/all_to_all | solution.py:224
  1072.0 220.8 %while.27 = (s32[]{:T(128)}, bf16[16,72,1024]{2,1,0:T(8,128)(2,1)S(1)}, bf16[16,72,1024]{2,1,0:T(8,128)(2,1)}, bf16[16,72,1024]{2,1,0:T(8,128)(2,1)}, bf16[16,72...) while((s32[]{:T(128)}, ...), condition=%wide.region_12.13_spmd, body=%wide.region_10.12_spmd.sunk | while | flops 767778816 | bytes 32969856 | solution.py:226
  1292.8 4.9 copy.127
  1297.7 6.4 copy.128
  1304.1 6.3 copy.129
  1310.4 6.9 pad_maximum_fusion
  1317.4 277.4 %all_to_all.66 = bf16[3,2,8,72,1024]{3,2,1,0,4:T(8,128)(2,1)} all-to-all(bf16[3,2,8,72,1024]{3,2,1,0,4:T(8,128)(2,1)S(1)} %pad_maximum_fusion), channel_id=1, replica_groups=mesh['fsdp'=4,'seq'=8] {'seq'}, dimensions={4} | all-to-all | bytes 14155776 | tf_op jit(solution)/shard_map/all_to_all | solution.py:231
  1594.8 15.4 copy.134
  1610.2 13.9 fusion.63
  1624.1 11.6 copy.135
  1637.6 11.5 copy.132
  1649.1 13.5 copy.153
  1662.6 4.2 convert_reduce_fusion
  1677.5 5.5 fusion.98
  1683.1 8.9 fusion.109
  1696.2 18.6 all-reduce.16
  1718.7 6.5 add_convert_fusion
  1725.3 19.0 fusion.94
  1747.5 29.3 %all-reduce.14 = (bf16[288]{0:T(512)(128)(2,1)S(1)}, bf16[288]{0:T(512)(128)(2,1)S(1)}, bf16[2,288]{1,0:T(2,128)(2,1)S(1)}, bf16[288]{0:T(512)(128)(2,1)S(1)}, b...) all-reduce(bf16[288]{0:T(512)(128)(2,1)S(1)} %dynamic-slice.8, ...), channel_id=1, replica_groups=mesh['fsdp'=4,'seq'=8] {'seq'}, use_global_device_ids=true, to_apply=%region_17.18 | all-reduce | flops 3380 | bytes 13520 | tf_op jit(solution)/shard_map/psum | solution.py:320
  1781.5 130.0 %all-reduce.20.cloned.1.call-done = (bf16[288,3456]{1,0:T(8,128)(2,1)}, bf16[288,1152]{1,0:T(8,128)(2,1)}, bf16[288,4304]{1,0:T(8,128)(2,1)}, bf16[4304,288]{0,1:T(8,128)(2,1)}) async-done(((bf16[288,3456]{1,0:T(8,128)(2,1)}, bf16[288,1152]{1,0:T(8,128)(2,1)}, bf16[288,4304]{1,0:T(8,128)(2,1)}, bf16[4304,288]{0,1:T(8,128)(2,1)}), (bf16[288,3456]{1,0:T(8,128)(2,1)}, bf16[288,1152]{1,0:T(8,128)(2,1)}, ...) | async-done | bytes 7612432 | tf_op jit(solution)/shard_map/psum | solution.py:322
  1911.5 4.5 convert_element_type.213
  (501 shorter events, 446.4 us)
Async XLA Ops:
  7.2 76.0 %copy-start.33 = (u32[32]{0:T(128)S(1)}, u32[32]{0:T(128)}, u32[]{:S(2)}) copy-start(u32[32]{0:T(128)} %constant.119) | copy-start | bytes 388
  7.2 77.9 %copy-start.35 = (bf16[288]{0:T(512)(128)(2,1)S(1)}, bf16[288]{0:T(512)(128)(2,1)}, u32[]{:S(2)}) copy-start(bf16[288]{0:T(512)(128)(2,1)} %param.22) | copy-start | bytes 1732
  7.2 78.1 %copy-start.36 = (bf16[288]{0:T(512)(128)(2,1)S(1)}, bf16[288]{0:T(512)(128)(2,1)}, u32[]{:S(2)}) copy-start(bf16[288]{0:T(512)(128)(2,1)} %param.23) | copy-start | bytes 1732
  7.2 78.4 %copy-start.37 = (bf16[288]{0:T(512)(128)(2,1)S(1)}, bf16[288]{0:T(512)(128)(2,1)}, u32[]{:S(2)}) copy-start(bf16[288]{0:T(512)(128)(2,1)} %param.27) | copy-start | bytes 1732
  7.2 78.6 %copy-start.38 = (bf16[288]{0:T(512)(128)(2,1)S(1)}, bf16[288]{0:T(512)(128)(2,1)}, u32[]{:S(2)}) copy-start(bf16[288]{0:T(512)(128)(2,1)} %param.28) | copy-start | bytes 1732
  7.2 78.9 %copy-start.39 = (bf16[288]{0:T(512)(128)(2,1)S(1)}, bf16[288]{0:T(512)(128)(2,1)}, u32[]{:S(2)}) copy-start(bf16[288]{0:T(512)(128)(2,1)} %param.29) | copy-start | bytes 1732
  7.2 79.1 %copy-start.32 = (bf16[1076]{0:T(1024)(128)(2,1)S(1)}, bf16[1076]{0:T(1024)(128)(2,1)}, u32[]{:S(2)}) copy-start(bf16[1076]{0:T(1024)(128)(2,1)} %param.31) | copy-start | bytes 6460
  7.3 229.8 %copy-start.34 = (bf16[2,288]{1,0:T(2,128)(2,1)S(1)}, bf16[2,288]{1,0:T(2,128)(2,1)}, u32[]{:S(2)}) copy-start(bf16[2,288]{1,0:T(2,128)(2,1)} %param.25) | copy-start | bytes 3460
  7.3 870.2 %all-gather.6.cloned.1.call-start = ((), (), s32[]{:S(2)}) async-start(), calls=%async_computation.9 | async-start | bytes 3317760 | tf_op jit(solution)/shard_map/all_gather | solution.py:133
  8.0 878.8 %all-gather.8.cloned.1.call-start = ((), (), s32[]{:S(2)}) async-start(), calls=%async_computation.10 | async-start | bytes 12533760 | tf_op jit(solution)/shard_map/all_gather | solution.py:175
  8.0 69.8 %collective-permute-start = (bf16[288,3456]{1,0:T(8,128)(2,1)}, bf16[288,3456]{1,0:T(8,128)(2,1)}, u32[]{:S(2)}, u32[]{:S(2)}) collective-permute-start(bf16[288,3456]{1,0:T(8,128)(2,1)} %param.24), channel_id=1, source_target_pairs={{0,8},{8,16},{16,24},{24,0},{1,9},{9,17},{17,25},{25,1},{2,10},{10... | collective-permute-start | bytes 5971976 | tf_op jit(solution)/shard_map/ppermute | solution.py:20
  11.1 295.7 %collective-permute-start.1 = (bf16[288,3456]{1,0:T(8,128)(2,1)}, bf16[288,3456]{1,0:T(8,128)(2,1)}, u32[]{:S(2)}, u32[]{:S(2)}) collective-permute-start(bf16[288,3456]{1,0:T(8,128)(2,1)} %param.24), channel_id=1, source_target_pairs={{0,24},{8,0},{16,8},{24,16},{1,25},{9,1},{17,9},{25,17},{2,26},{10... | collective-permute-start | bytes 5971976 | tf_op jit(solution)/shard_map/ppermute | solution.py:23
  77.9 260.9 %collective-permute-start.2 = (bf16[288,3456]{1,0:T(8,128)(2,1)}, bf16[288,3456]{1,0:T(8,128)(2,1)}, u32[]{:S(2)}, u32[]{:S(2)}) collective-permute-start(bf16[288,3456]{1,0:T(8,128)(2,1)} %collective-permute-done), channel_id=1, source_target_pairs={{0,8},{8,16},{16,24},{24,0},{1,9},{9,17},{17,25},{25,1},{2,10},{10... | collective-permute-start | bytes 5971976 | tf_op jit(solution)/shard_map/ppermute | solution.py:20
  237.1 133.6 %copy-start.15 = (f32[1152]{0:T(1024)}, f32[1152]{0:T(1024)S(1)}, u32[]{:S(2)}) copy-start(f32[1152]{0:T(1024)S(1)} %convert_element_type.178) | copy-start | bytes 13828
  237.1 133.6 %copy-start.28 = (f32[1152]{0:T(1024)}, f32[1152]{0:T(1024)S(1)}, u32[]{:S(2)}) copy-start(f32[1152]{0:T(1024)S(1)} %convert_element_type.179) | copy-start | bytes 13828
  245.6 28.2 %copy-start.2 = (bf16[8,128,1152]{2,1,0:T(8,128)(2,1)S(1)}, bf16[8,128,1152]{2,1,0:T(8,128)(2,1)}, u32[]{:S(2)}) copy-start(bf16[8,128,1152]{2,1,0:T(8,128)(2,1)} %param.20) | copy-start | bytes 7077892
  274.2 96.4 %copy-start.17 = (f32[8,128]{1,0:T(8,128)}, f32[8,128]{1,0:T(8,128)S(1)}, u32[]{:S(2)}) copy-start(f32[8,128]{1,0:T(8,128)S(1)} %broadcast_multiply_fusion.1) | copy-start | bytes 12292
  275.6 95.0 %copy-start.21 = (f32[8,128]{1,0:T(8,128)}, f32[8,128]{1,0:T(8,128)S(1)}, u32[]{:S(2)}) copy-start(f32[8,128]{1,0:T(8,128)S(1)} %fusion.107) | copy-start | bytes 12292
  389.7 6.0 copy-start.41
  389.7 161.2 %all-to-all-start = ((bf16[3,16,8,72,128]{4,3,2,0,1:T(8,128)(2,1)}), bf16[3,16,8,72,128]{4,3,2,0,1:T(8,128)(2,1)}, u32[]{:S(2)}, u32[]{:S(2)}) async-start(bf16[3,16,8,72,128]{4,3,2,0,1:T(8,128)(2,1)} %copy.118), calls=%async_computation | async-start | bytes 14155776 | tf_op jit(solution)/shard_map/all_to_all | solution.py:149
  395.0 516.6 %all-gather.10.cloned.1.call-start = ((), (), s32[]{:S(2)}) async-start(), calls=%async_computation.11 | async-start | bytes 12533760 | tf_op jit(solution)/shard_map/all_gather | solution.py:177
  600.5 2.0 copy-start
  656.7 2.0 copy-start
  690.5 2.0 copy-start
  724.2 2.0 copy-start
  766.2 6.3 copy-start.42
  772.6 98.5 %all-to-all-start.1 = ((bf16[2,8,72,1024]{2,1,0,3:T(8,128)(2,1)}), bf16[2,8,72,1024]{2,1,0,3:T(8,128)(2,1)}, u32[]{:S(2)}, u32[]{:S(2)}) async-start(bf16[2,8,72,1024]{2,1,0,3:T(8,128)(2,1)} %bitcast.255), calls=%async_computation.1 | async-start | bytes 8388608 | tf_op jit(solution)/shard_map/all_to_all | solution.py:159
  777.1 860.4 %all-gather.12.cloned.1.call-start = ((), (), s32[]{:S(2)}) async-start(), calls=%async_computation.12 | async-start | bytes 9953280 | tf_op jit(solution)/shard_map/all_gather | solution.py:196
  777.7 937.7 %reduce-scatter.10.cloned.1.call-start = ((), (), s32[]{:S(2)}) async-start(), calls=%async_computation.14 | async-start | bytes 3317760 | tf_op jit(solution)/shard_map/reduce_scatter | solution.py:281
  883.9 2.2 copy-start.5
  886.8 57.3 %slice-start = ((s8[4718592]{0:T(1024)(128)(4,1)}), s8[524288]{0:T(1024)(128)(4,1)S(1)}, s32[]{:S(2)}) async-start(s8[4718592]{0:T(1024)(128)(4,1)} %bitcast.253), calls=%async_computation.19 | async-start | bytes 1048576
  911.6 32.5 %slice-start.1 = ((s8[4718592]{0:T(1024)(128)(4,1)}), s8[4194304]{0:T(1024)(128)(4,1)S(1)}, s32[]{:S(2)}) async-start(s8[4718592]{0:T(1024)(128)(4,1)} %bitcast.253), calls=%async_computation.20 | async-start | bytes 8388608
  964.7 3.3 copy-start.7
  967.9 2.4 copy-start.4
  968.0 2.4 copy-start.19
  968.0 3.8 copy-start.9
  976.2 739.1 %reduce-scatter.12.cloned.1.call-start = ((), (), s32[]{:S(2)}) async-start(), calls=%async_computation.15 | async-start | bytes 12533760 | tf_op jit(solution)/shard_map/reduce_scatter | solution.py:293
  1001.9 6.2 copy-start.8
  1003.7 59.0 %all-to-all-start.2 = ((bf16[16,8,72,128]{3,2,1,0:T(8,128)(2,1)}), bf16[16,8,72,128]{3,2,1,0:T(8,128)(2,1)}, u32[]{:S(2)}, u32[]{:S(2)}) async-start(bf16[16,8,72,128]{3,2,1,0:T(8,128)(2,1)} %copy.125), calls=%async_computation.2 | async-start | bytes 4718592 | tf_op jit(solution)/shard_map/all_to_all | solution.py:224
  1008.0 707.3 %reduce-scatter.14.cloned.1.call-start = ((), (), s32[]{:S(2)}) async-start(), calls=%async_computation.16 | async-start | bytes 12533760 | tf_op jit(solution)/shard_map/reduce_scatter | solution.py:299
  1024.8 693.9 %reduce-scatter.8.cloned.1.call-start = ((), (), s32[]{:S(2)}) async-start(), calls=%async_computation.13 | async-start | bytes 9953280 | tf_op jit(solution)/shard_map/reduce_scatter | solution.py:275
  1068.3 3.7 copy-start.43
  1594.7 15.4 copy-start.3
  1594.7 15.4 copy-start.16
  1594.7 15.4 copy-start.18
  1594.7 15.4 copy-start.22
  1594.7 15.4 copy-start.29
  1594.8 15.4 copy-start.44
  1635.7 110.8 %reduce-scatter.16.cloned.1.call-start = ((), (), s32[]{:S(2)}) async-start(), calls=%async_computation.17 | async-start | bytes 368640
  1662.6 5.4 copy-start.1
  1673.4 3.1 copy-start.6
  1676.5 6.6 slice-start.2
  1677.5 5.5 slice-start.3
  1683.1 8.9 copy-start.24
  1692.0 4.2 copy-start.25
  1692.0 4.2 copy-start.26
  1692.0 4.2 copy-start.27
  1692.0 4.2 copy-start.30
  1692.0 4.2 copy-start.31
  1692.1 219.4 %all-reduce.20.cloned.1.call-start = ((), (), s32[]{:S(2)}) async-start(), calls=%async_computation.18 | async-start | bytes 15335424 | tf_op jit(solution)/shard_map/psum | solution.py:322
  1696.1 22.6 %copy-start.20 = (f32[8,128]{1,0:T(8,128)S(1)}, f32[8,128]{1,0:T(8,128)}, u32[]{:S(2)}) copy-start(f32[8,128]{1,0:T(8,128)} %copy-done.19) | copy-start | bytes 12292
  1911.5 4.5 copy-start.11
  1915.9 2.6 copy-start.13
  1918.5 2.2 copy-start.14
  (16 other events, 29.5 us)
Sparse Core Ops, SparseCore 0:
  9.9 64.6 all-gather.5
  79.1 165.3 all-gather.7
  397.7 101.6 all-gather.9
  779.5 84.3 all-gather.11
  976.4 37.7 reduce-scatter.9
  1017.2 99.6 reduce-scatter.11
  1120.1 99.6 reduce-scatter.13
  1635.8 82.8 reduce-scatter.7
  1722.1 24.3 reduce-scatter.15
  1749.0 162.4 all-reduce.19
